TPU v7x, 128 devices: a whole 4x4x4 slice. The times are simulated.
128 devices in a mesh: blk: 16 (over z_lo, y, core), seq: 8 (over x, z_hi).
Axes of the slice: x: 4, y: 4, z: 4 (z_hi: 2, z_lo: 2; z = z_hi * 2 + z_lo), core: 2. Of those that a mesh axis runs over, the one named last changes fastest.
Arguments:
- layer_input: bfloat16 [16, 1024, 8192], P('blk', 'seq'), may hold values from -6 to 6
- queries: bfloat16 [16, 1024, 4096], P('blk', 'seq'), may hold values from -48 to 48, as said below
- grad_out: bfloat16 [16, 1024, 4096], P('blk', 'seq'), may hold values from -6 to 6
- segment_ids: int32 [16, 1024], P('blk', 'seq'), may hold values from 0 to 3, never falling along the last dimension, each value on 1 to 512 neighbouring positions
- kv_weight: bfloat16 [8192, 1024], P(('blk', 'seq')), may hold values from -0.0625 to 0.0625
- norm_gain: float32 [8192], replicated, may hold values from 0.5 to 1.5
Outputs:
- attended: bfloat16 [16, 1024, 4096], P('blk', 'seq')
- grad_queries: bfloat16 [16, 1024, 4096], P('blk', 'seq')
- grad_input: bfloat16 [16, 1024, 8192], P('blk', 'seq')
- grad_weight: float32 [8192, 1024], P(('blk', 'seq'))
- grad_gain: float32 [8192], replicated
Inputs may be any that keep to these rules, and one draw needn't show every extreme that they name: Projected queries; some rows may be larger than others.
All inputs are finite; a program needn't handle non-finite values.
Results may differ from a plain program's by a relative error of at most 0.02.
The roundings to bfloat16 on the way count: a program that leaves them out, or rounds other values in their place, can miss the bound.
Values may be sent and summed in bfloat16 or wider, within the bound.
No kernel may reach another device: no remote copies, remote signals or barrier semaphores. Data moves between devices by JAX's collectives and lax.ppermute only.
A program may use at most 128 MiB of HBM per device.

v0:
```python
import jax
import jax.numpy as jnp
from jax import lax
from jax.sharding import PartitionSpec as P

HEAD = 128
epsilon = 1e-05


def cut_along(shard, dim, length):
    lengths = shard.shape
    pieces = shard.reshape(*lengths[:dim], length, lengths[dim] // length, *lengths[dim + 1 :])
    return jnp.moveaxis(pieces, dim, 0)


def sum_at_owner(shard, axis, dim):
    length = lax.axis_size(axis)
    pieces = lax.all_to_all(cut_along(shard, dim, length), axis, 0, 0, tiled=True)
    return jnp.sum(pieces, axis=0)


def shards(layer_input, queries, grad_out, segment_ids, kv_weight, norm_gain):
    f32 = jnp.float32
    tok_rows = layer_input.shape[1]
    model_width = layer_input.shape[2]
    seq_devices = lax.axis_size("seq")
    blk_devices = lax.axis_size("blk")
    length = tok_rows * seq_devices
    seq_index = lax.axis_index("seq")
    kv_total = kv_weight.shape[1]
    kv_width = kv_total // 2
    kv_heads = kv_width // HEAD
    query_count = queries.shape[2] // HEAD
    group_size = query_count // kv_heads
    score_scale = HEAD ** (-0.5)
    piece_cols = kv_weight.shape[0]
    source = layer_input[0].astype(f32)
    inv_rms = lax.rsqrt(jnp.mean(source * source, axis=1, keepdims=True) + epsilon)
    scaled = source * inv_rms
    normed = (scaled * norm_gain).astype(jnp.bfloat16)
    split_cols = normed.reshape(tok_rows, blk_devices, seq_devices, piece_cols)
    columns = lax.all_to_all(split_cols, "seq", split_axis=2, concat_axis=0, tiled=True).reshape(
        length, blk_devices * piece_cols
    )
    weight_slab = lax.all_gather(kv_weight, "blk", axis=0, tiled=True)
    query_heads = queries[0].reshape(tok_rows, kv_heads, group_size, HEAD)
    query_pos = seq_index * tok_rows + jnp.arange(tok_rows, dtype=jnp.int32)
    query_doc = segment_ids[0]
    grad_heads = grad_out[0].reshape(tok_rows, kv_heads, group_size, HEAD).transpose(1, 2, 0, 3)

    def scores_of(kv_piece, doc_piece):
        rows_here = kv_piece.shape[0]
        key_heads = kv_piece[:, :kv_width].reshape(rows_here, kv_heads, HEAD)
        raw_scores = (
            jnp.einsum("qgjd,kgd->gjqk", query_heads, key_heads, preferred_element_type=f32)
            * score_scale
        )
        key_pos = jnp.arange(rows_here, dtype=jnp.int32)
        allowed = (key_pos[None, :] <= query_pos[:, None]) & (
            doc_piece[None, :] == query_doc[:, None]
        )
        return (jnp.where(allowed, raw_scores, -1e30), allowed, key_heads)

    stat_shape = (kv_heads, group_size, tok_rows, 1)
    kv_own = sum_at_owner(
        jnp.dot(columns, weight_slab, preferred_element_type=f32), "seq", 0
    ).astype(jnp.bfloat16)
    row_max = jnp.full(stat_shape, -1e30, f32)
    kv_piece = lax.all_gather(kv_own, "seq", axis=0, tiled=True)
    doc_piece = lax.all_gather(query_doc, "seq", axis=0, tiled=True)
    rows_here = kv_piece.shape[0]
    masked, allowed, key_heads = scores_of(kv_piece, doc_piece)
    new_max = jnp.maximum(row_max, jnp.max(masked, axis=-1, keepdims=True))
    expo_terms = jnp.where(allowed, jnp.exp(masked - new_max), 0.0)
    value_heads = kv_piece[:, kv_width:].reshape(rows_here, kv_heads, HEAD)
    weights = expo_terms.astype(jnp.bfloat16)
    weighted = jnp.einsum("gjqk,kgd->gjqd", weights, value_heads, preferred_element_type=f32)
    row_sum = jnp.sum(expo_terms, axis=-1, keepdims=True)
    row_max, row_sum, weighted = (new_max, row_sum, weighted)
    summed = weighted / row_sum
    attended = (
        summed.transpose(2, 0, 1, 3).reshape(tok_rows, query_count * HEAD).astype(jnp.bfloat16)
    )
    log_total = row_max + jnp.log(row_sum)
    attended_heads = attended.reshape(tok_rows, kv_heads, group_size, HEAD).transpose(1, 2, 0, 3)
    row_delta = jnp.sum(grad_heads.astype(f32) * attended_heads.astype(f32), axis=-1, keepdims=True)
    kv_piece = lax.all_gather(kv_own, "seq", axis=0, tiled=True)
    doc_piece = lax.all_gather(query_doc, "seq", axis=0, tiled=True)
    rows_here = kv_piece.shape[0]
    masked, allowed, key_heads = scores_of(kv_piece, doc_piece)
    softmax_probs = jnp.where(allowed, jnp.exp(masked - log_total), 0.0)
    value_heads = kv_piece[:, kv_width:].reshape(rows_here, kv_heads, HEAD)
    grad_probs = jnp.einsum("gjqd,kgd->gjqk", grad_heads, value_heads, preferred_element_type=f32)
    grad_scores = (softmax_probs * (grad_probs - row_delta)).astype(jnp.bfloat16)
    probs_half = softmax_probs.astype(jnp.bfloat16)
    grad_values = jnp.einsum("gjqk,gjqd->kgd", probs_half, grad_heads, preferred_element_type=f32)
    grad_keys = (
        jnp.einsum("gjqk,qgjd->kgd", grad_scores, query_heads, preferred_element_type=f32)
        * score_scale
    )
    grad_query = (
        jnp.einsum("gjqk,kgd->qgjd", grad_scores, key_heads, preferred_element_type=f32)
        * score_scale
    )
    new_rows = jnp.concatenate(
        [grad_keys.reshape(rows_here, kv_width), grad_values.reshape(rows_here, kv_width)], axis=1
    )
    grad_rows = new_rows
    grad_query, grad_rows = (grad_query, grad_rows)
    grad_own = sum_at_owner(grad_rows, "seq", 0).astype(jnp.bfloat16)
    grad_kv = lax.all_gather(grad_own, "seq", axis=0, tiled=True)
    grad_queries = grad_query.reshape(tok_rows, query_count * HEAD).astype(jnp.bfloat16)
    slab_back = lax.all_gather(kv_weight, "blk", axis=0, tiled=True)
    grad_weight = lax.psum_scatter(
        lax.dot_general(columns, grad_kv, (((0,), (0,)), ((), ())), preferred_element_type=f32),
        "blk",
        scatter_dimension=0,
        tiled=True,
    )
    grad_cols = lax.dot_general(
        grad_kv, slab_back, (((1,), (1,)), ((), ())), preferred_element_type=f32
    ).astype(jnp.bfloat16)
    grad_cols = grad_cols.reshape(length, blk_devices, 1, piece_cols)
    grad_normed = lax.all_to_all(grad_cols, "seq", split_axis=0, concat_axis=2, tiled=True).reshape(
        tok_rows, model_width
    )
    grad_norm = grad_normed.astype(f32)
    grad_gain = lax.psum(jnp.sum(grad_norm * scaled, axis=0), ("blk", "seq"))
    grad_hat = grad_norm * norm_gain
    grad_input = inv_rms * (grad_hat - scaled * jnp.mean(grad_hat * scaled, axis=1, keepdims=True))
    return (
        attended[None],
        grad_queries[None],
        grad_input.astype(jnp.bfloat16)[None],
        grad_weight,
        grad_gain,
    )


def solution(mesh):
    in_specs = (
        P("blk", "seq", None),
        P("blk", "seq", None),
        P("blk", "seq", None),
        P("blk", "seq"),
        P(("blk", "seq"), None),
        P(),
    )
    out_specs = (
        P("blk", "seq", None),
        P("blk", "seq", None),
        P("blk", "seq", None),
        P(("blk", "seq"), None),
        P(),
    )
    return jax.shard_map(shards, mesh=mesh, in_specs=in_specs, out_specs=out_specs, check_vma=False)
```

profile of v0, /device:TPU:1, one launch (start us, length us, event | category | flops | bytes accessed | tf_op | source)
XLA Modules:
  0.0 534.6 jit_solution(473694179402004484)
XLA Ops:
  7.2 0.0 all-gather.5.cloned.1.call-start
  7.2 0.7 all-gather.5.cloned.1.call-update
  7.9 0.0 all-gather.7.cloned.1.call-start
  8.0 3.2 copy.148
  11.2 2.2 convert_element_type.140
  13.4 0.1 mul.121
  13.5 1.1 multiply_reduce_fusion.2
  14.6 2.9 multiply_convert_fusion
  17.5 0.2 copy.149
  17.7 38.3 %all_to_all.34 = bf16[128,16,8,64]{0,3,1,2:T(8,128)(2,1)} all-to-all(bf16[128,16,8,64]{0,3,1,2:T(8,128)(2,1)S(1)} %copy.149), channel_id=1, replica_groups=mesh['blk'=16,'seq'=8] {'seq'}, dimensions={2} | all-to-all | bytes 4194304 | tf_op jit(solution)/shard_map/all_to_all | solution.py:42
  56.0 8.3 %all-gather.5.cloned.1.call-done = bf16[1024,1024]{1,0:T(8,128)(2,1)} async-done(((bf16[64,1024]{1,0:T(8,128)(2,1)}), bf16[1024,1024]{1,0:T(8,128)(2,1)}) %all-gather.5.cloned.1.call-update) | async-done | bytes 2097168 | tf_op jit(solution)/shard_map/all_gather | solution.py:45
  64.3 4.6 fusion.22
  68.9 55.1 %all_to_all.35 = f32[8,128,1024]{2,1,0:T(8,128)} all-to-all(f32[8,128,1024]{2,1,0:T(8,128)S(1)} %fusion.22), channel_id=1, replica_groups=mesh['blk'=16,'seq'=8] {'seq'}, dimensions={0} | all-to-all | bytes 8388608 | tf_op jit(solution)/shard_map/all_to_all | solution.py:18
  124.1 3.4 reduce_sum.66
  127.5 0.0 all-gather.9.cloned.1.call-start
  127.6 1.2 copy.192
  128.8 2.3 copy.156
  131.0 17.1 %all-gather = s32[1,1024]{1,0:T(1,128)S(1)} all-gather(s32[1,128]{1,0:T(1,128)S(1)} %copy-done.8), channel_id=2, replica_groups=mesh['blk'=16,'seq'=8] {'seq'}, dimensions={1}, use_global_device_ids=true | all-gather | bytes 4608 | tf_op jit(solution)/shard_map/all_gather | solution.py:70
  148.2 0.2 fusion.29
  148.4 30.2 %all-gather.7.cloned.1.call-done = bf16[1024,1024]{1,0:T(8,128)(2,1)} async-done(((bf16[128,1024]{1,0:T(8,128)(2,1)}), bf16[1024,1024]{1,0:T(8,128)(2,1)}) %all-gather.7.cloned.1.call-update) | async-done | bytes 2097168 | tf_op jit(solution)/shard_map/all_gather | solution.py:69
  178.5 3.0 fusion.32
  181.5 1.5 copy.151
  183.0 9.1 %fusion.33 = (f32[4,8,128]{2,1,0:T(8,128)S(1)}, f32[4,8,128,1024]{2,3,1,0:T(8,128)}) fusion(bf16[1024,4,128,1]{0,2,3,1:T(8,128)(2,1)S(1)} %bitcast.122, bf16[128,4,8,128]{3,2,1,0:T(8,128)(2,1)} %bitcast.124, pred[128,1024]{0,1:T(8,128)(4,1)S(1)} %fusion.29), kind=kOutput, calls=%fused_computation.52 | convolution fusion | flops 1086320640 | bytes 19021824 | tf_op jit(solution)/shard_map/qgjd,kgd->gjqk/dot_general | solution.py:55
  192.1 2.3 copy.154
  194.4 8.7 %fusion.1 = f32[4,8,128]{2,1,0:T(8,128)S(1)} fusion(f32[4,8,128,1024]{2,3,1,0:T(8,128)} %get-tuple-element.45, f32[4,8,128]{2,1,0:T(8,128)S(1)} %broadcast_maximum_fusion, pred[128,1024]{0,1:T(8,128)(4,1)S(1)} %fusion.29), kind=kLoop, calls=%fused_computation.5 | loop fusion | flops 12578816 | bytes 16941056 | tf_op jit(solution)/shard_map/reduce_sum | solution.py:78
  203.1 9.9 %fusion.21 = (bf16[128,4,8,128]{0,3,2,1:T(8,128)(2,1)}, f32[4,8,128,128]{2,3,1,0:T(8,128)S(1)}) fusion(f32[128,4,8]{0,2,1:T(8,128)S(1)} %bitcast.140, bf16[1024,4,128,1]{0,2,3,1:T(8,128)(2,1)S(1)} %bitcast.138, f32[4,8,128,1024]{2,3,1,0:T(8,128)} %get-tuple-element.45, f32[4,8,128]{2,1,0:T(8,128)S(1)} %broadcast_maximum_fusion, ...), kind=kOutput, calls=%fused_computation.32 | convolution fusion | flops 1087373312 | bytes 21135360 | tf_op jit(solution)/shard_map/gjqk,kgd->gjqd/dot_general | solution.py:77
  212.9 0.5 multiply_reduce_fusion.3
  213.4 9.5 %fusion.24 = f32[1024,4,128]{2,0,1:T(8,128)} fusion(bf16[4,8,128,128]{2,3,1,0:T(8,128)(2,1)S(1)} %bitcast.131, f32[4,8,128,1024]{2,3,1,0:T(8,128)} %get-tuple-element.45, f32[4,8,128]{2,1,0:T(8,128)S(1)} %log_add_fusion, pred[128,1024]{0,1:T(8,128)(4,1)S(1)} %fusion.29), kind=kOutput, calls=%fused_computation.39 | convolution fusion | flops 1086324736 | bytes 20070400 | tf_op jit(solution)/shard_map/gjqk,gjqd->kgd/dot_general | solution.py:96
  222.9 10.9 %fusion = bf16[4,8,128,1024]{2,3,1,0:T(8,128)(2,1)} fusion(f32[4,8,128,1024]{2,3,1,0:T(8,128)} %get-tuple-element.45, bf16[1024,4,128,1]{0,2,3,1:T(8,128)(2,1)S(1)} %bitcast.139, bf16[4,8,128,128]{2,3,1,0:T(8,128)(2,1)S(1)} %bitcast.132, f32[4,8,128]{2,1,0:T(8,128)S(1)} %multiply_reduce_fusion.3, f32[4,8,128]{2,1,0:T(8,128)S(1)} %log_add_fusion, ...), kind=kOutput, calls=%fused_computation.1 | convolution fusion | flops 1094713344 | bytes 27426816 | tf_op jit(solution)/shard_map/gjqd,kgd->gjqk/dot_general | solution.py:93
  233.8 2.9 copy.163
  236.7 3.5 copy.194
  240.2 7.1 %fusion.20 = f32[1024,4,128]{2,0,1:T(8,128)} fusion(bf16[4,8,128,1024]{2,3,1,0:T(8,128)(2,1)} %fusion, bf16[128,4,8,128]{3,2,1,0:T(8,128)(2,1)S(1)} %bitcast.125), kind=kOutput, calls=%fused_computation.30 | convolution fusion | flops 1074266112 | bytes 11534336 | tf_op jit(solution)/shard_map/gjqk,qgjd->kgd/dot_general | solution.py:98
  247.3 2.9 copy.161
  250.2 2.2 copy.193
  252.4 0.3 pad_maximum_fusion
  252.7 0.8 copy.164
  253.5 50.9 %all_to_all.36 = f32[8,128,1024]{1,2,0:T(8,128)} all-to-all(f32[8,128,1024]{1,2,0:T(8,128)S(1)} %copy.164), channel_id=1, replica_groups=mesh['blk'=16,'seq'=8] {'seq'}, dimensions={0} | all-to-all | bytes 8388608 | tf_op jit(solution)/shard_map/all_to_all | solution.py:18
  304.4 3.2 reduce_sum.69
  307.6 0.2 reduce-scatter.2.cloned.1.call-start
  307.8 4.7 copy.171
  312.5 51.4 %all-gather.9.cloned.1.call-done = bf16[1024,1024]{0,1:T(8,128)(2,1)} async-done(((bf16[128,1024]{0,1:T(8,128)(2,1)}), bf16[1024,1024]{0,1:T(8,128)(2,1)}) %all-gather.9.cloned.1.call-update) | async-done | bytes 2097168 | tf_op jit(solution)/shard_map/all_gather | solution.py:111
  363.9 6.5 %fusion.17 = f32[1024,1024]{1,0:T(8,128)} fusion(bf16[1024,1024]{0,1:T(8,128)(2,1)} %all-gather.9.cloned.1.call-done, bf16[128,8,8,128]{3,2,1,0:T(8,128)(2,1)} %bitcast.135), kind=kOutput, calls=%fused_computation.26 | convolution fusion | flops 2147483648 | bytes 8388608 | tf_op jit(solution)/shard_map/dot_general | solution.py:115
  370.4 5.9 %convolution_convert_fusion = bf16[1024,1024]{0,1:T(8,128)(2,1)} fusion(bf16[1024,1024]{1,0:T(8,128)(2,1)} %all-gather.5.cloned.1.call-done, bf16[1024,1024]{0,1:T(8,128)(2,1)} %all-gather.9.cloned.1.call-done), kind=kOutput, calls=%fused_computation.38 | convolution fusion | flops 2148532224 | bytes 6291456 | tf_op jit(solution)/shard_map/dot_general | solution.py:120
  376.3 6.2 %copy.166 = bf16[1024,16,1,64]{3,1,2,0:T(8,128)(2,1)} copy(bf16[1024,16,1,64]{0,3,1,2:T(8,128)(2,1)} %bitcast.134) | data formatting | bytes 4194304 | tf_op jit(solution)/shard_map/reshape | solution.py:123
  382.5 7.6 %reshape.223 = bf16[8,2,65536]{2,1,0:T(2,128)(2,1)} reshape(bf16[1024,1,16,64]{3,2,1,0:T(8,128)(2,1)} %bitcast.119) | data formatting | bytes 4194304
  390.1 4.6 all-to-all-start.3
  394.6 1.0 copy.169
  395.7 2.3 copy.173
  397.9 5.6 %multiply_convert_fusion.1 = bf16[4,128,8,128]{3,1,2,0:T(8,128)(2,1)} fusion(bf16[1024,4,128,1]{0,2,3,1:T(8,128)(2,1)S(1)} %bitcast.123, bf16[4,8,128,1024]{2,3,1,0:T(8,128)(2,1)} %fusion), kind=kOutput, calls=%fused_computation.35 | convolution fusion | flops 1074790400 | bytes 10485760 | tf_op jit(solution)/shard_map/gjqk,kgd->qgjd/dot_general | solution.py:102
  403.6 2.3 copy.174
  405.9 22.6 %all-to-all-done.3 = bf16[8,2,65536]{2,1,0:T(2,128)(2,1)} async-done(((bf16[8,2,65536]{2,1,0:T(2,128)(2,1)}), bf16[8,2,65536]{2,1,0:T(2,128)(2,1)}, u32[]{:S(2)}, u32[]{:S(2)}) %all-to-all-start.3) | async-done | bytes 2097184 | tf_op jit(solution)/shard_map/all_to_all | solution.py:124
  428.4 7.4 %reshape.224 = bf16[1024,1,16,64]{3,2,1,0:T(8,128)(2,1)} reshape(bf16[8,2,65536]{2,1,0:T(2,128)(2,1)} %all-to-all-done.3) | data formatting | bytes 4194304
  435.8 5.5 %copy.167 = bf16[1024,16,1,64]{0,3,2,1:T(8,128)(2,1)} copy(bf16[1024,16,1,64]{3,1,2,0:T(8,128)(2,1)} %bitcast.120) | data formatting | bytes 4194304 | tf_op jit(solution)/shard_map/all_to_all | solution.py:124
  441.3 2.1 convert_element_type.146
  443.4 1.0 copy.195
  444.4 0.7 copy.168
  445.2 1.4 copy-done
  446.6 0.1 copy-done.4
  446.7 4.8 multiply_reduce_fusion
  451.5 4.4 fusion.16
  455.9 4.1 copy.175
  460.0 0.2 copy.172
  460.2 0.1 reduce_sum.72
  460.2 67.6 %psum.7 = f32[8192]{0:T(1024)} all-reduce(f32[8192]{0:T(1024)S(1)} %reduce_sum.72), channel_id=1, replica_groups=mesh['blk'=16,'seq'=8] {'blk','seq'}, use_global_device_ids=true, to_apply=%region_9.10 | all-reduce | flops 8192 | bytes 65536 | tf_op jit(solution)/shard_map/psum | solution.py:128
  (25 shorter events, 0.1 us)
Async XLA Ops:
  7.2 57.1 %all-gather.5.cloned.1.call-start = ((), (), s32[]{:S(2)}) async-start(), calls=%async_computation.5 | async-start | bytes 2228224 | tf_op jit(solution)/shard_map/all_gather | solution.py:45
  7.9 5.5 %copy-start.7 = (f32[8192]{0:T(1024)S(1)}, f32[8192]{0:T(1024)}, u32[]{:S(2)}) copy-start(f32[8192]{0:T(1024)} %param.11) | copy-start | bytes 98308
  7.9 170.6 %all-gather.7.cloned.1.call-start = ((), (), s32[]{:S(2)}) async-start(), calls=%async_computation.6 | async-start | bytes 2359296 | tf_op jit(solution)/shard_map/all_gather | solution.py:69
  124.0 3.5 copy-start.5
  124.0 7.0 %copy-start.8 = (s32[1,128]{1,0:T(1,128)S(1)}, s32[1,128]{1,0:T(1,128)}, u32[]{:S(2)}) copy-start(s32[1,128]{1,0:T(1,128)} %param.9) | copy-start | bytes 1540
  127.5 236.4 %all-gather.9.cloned.1.call-start = ((), (), s32[]{:S(2)}) async-start(), calls=%async_computation.7 | async-start | bytes 2359296 | tf_op jit(solution)/shard_map/all_gather | solution.py:111
  194.4 8.7 %copy-start.6 = (bf16[1024,512]{0,1:T(8,128)(2,1)S(1)}, bf16[1024,512]{0,1:T(8,128)(2,1)}, u32[]{:S(2)}) copy-start(bf16[1024,512]{0,1:T(8,128)(2,1)} %copy.154) | copy-start | bytes 3145732
  203.1 9.9 %copy-start.3 = (bf16[1,128,4096]{1,2,0:T(8,128)(2,1)S(1)}, bf16[1,128,4096]{1,2,0:T(8,128)(2,1)}, u32[]{:S(2)}) copy-start(bf16[1,128,4096]{1,2,0:T(8,128)(2,1)} %copy.156) | copy-start | bytes 3145732
  236.7 3.5 copy-start.1
  250.2 2.2 copy-start.2
  307.6 220.3 %reduce-scatter.2.cloned.1.call-start = ((), (), s32[]{:S(2)}) async-start(), calls=%async_computation.8 | async-start | bytes 4456448 | tf_op jit(solution)/shard_map/reduce_scatter | solution.py:114
  390.1 38.4 %all-to-all-start.3 = ((bf16[8,2,65536]{2,1,0:T(2,128)(2,1)}), bf16[8,2,65536]{2,1,0:T(2,128)(2,1)}, u32[]{:S(2)}, u32[]{:S(2)}) async-start(bf16[8,2,65536]{2,1,0:T(2,128)(2,1)} %reshape.223), calls=%async_computation.3 | async-start | bytes 4194304 | tf_op jit(solution)/shard_map/all_to_all | solution.py:124
  444.4 2.2 copy-start
  444.4 2.3 copy-start.4
Sparse Core Ops, SparseCore 0:
  9.7 54.5 all-gather.4
  127.6 50.8 all-gather.6
  307.7 56.0 all-gather.8
  370.5 72.2 reduce-scatter.1
where the time goes:
time: 540 us; the launch traced here: 535 us
  blocking collectives  229 us (42%)
  waiting for transfers between devices  113 us (21%)
  local copies, waits for them, and re-layouts  70.6 us (13%)
  matrix products  69.1 us (13%)
  other arithmetic  33.7 us (6%)
  between operations  14.2 us (3%)
    all_to_all x2, blocking collectives, sum_at_owner(): lax.all_to_all(cut_along(shard, dim, length), axis, 0, 0, tiled=True)  106 us
    psum x1, blocking collectives, shards(): grad_gain = lax.psum(jnp.sum(grad_norm * scaled, axis=0), ('blk', 'seq'))  67.6 us
    all_gather x1, waiting for transfers between devices, shards(): grad_kv = lax.all_gather(grad_own, 'seq', axis=0, tiled=True)  51.4 us
    unnamed x29, local copies, waits for them, and re-layouts  38.6 us
    all_to_all x1, blocking collectives, shards(): lax.all_to_all(split_cols, 'seq', split_axis=2, concat_axis=0, tiled=True)  38.3 us
    all_gather x1, waiting for transfers between devices, shards(): kv_piece = lax.all_gather(kv_own, 'seq', axis=0, tiled=True)  30.2 us
    all_to_all x1, waiting for transfers between devices, shards(): lax.all_to_all(grad_cols, 'seq', split_axis=0, concat_axis=2, tiled=True)  22.6 us
    all_gather x1, blocking collectives, shards(): doc_piece = lax.all_gather(query_doc, 'seq', axis=0, tiled=True)  17.1 us
  transfers between devices with their start and end apart: 5, of which 4 were waited for; matrix products, arithmetic and copies ran while one was open for 15% of the time, Pallas kernels for 0%

commit v1 on v0

--- a/solution.py
+++ b/solution.py
@@ -5,6 +5,14 @@
 
 HEAD = 128
 epsilon = 1e-05
+
+
+def test_columns(sheet):
+    b_next = jax.lax.psum(1, axis_name="seq")
+    field_out = jnp.split(sheet, b_next, axis=0)
+    d_next = jnp.stack(field_out)
+    big = jax.lax.all_to_all(d_next, concat_axis=0, split_axis=0, axis_name="seq")
+    return jnp.concatenate(big, axis=2)
 
 
 def cut_along(shard, dim, length):
@@ -121,9 +129,7 @@
         grad_kv, slab_back, (((1,), (1,)), ((), ())), preferred_element_type=f32
     ).astype(jnp.bfloat16)
     grad_cols = grad_cols.reshape(length, blk_devices, 1, piece_cols)
-    grad_normed = lax.all_to_all(grad_cols, "seq", split_axis=0, concat_axis=2, tiled=True).reshape(
-        tok_rows, model_width
-    )
+    grad_normed = test_columns(grad_cols).reshape(tok_rows, model_width)
     grad_norm = grad_normed.astype(f32)
     grad_gain = lax.psum(jnp.sum(grad_norm * scaled, axis=0), ("blk", "seq"))
     grad_hat = grad_norm * norm_gain

time: 540 us -> 506 us (0.937)
  local copies, waits for them, and re-layouts: 70.6 us -> 45.6 us
    unnamed x29, local copies, waits for them, and re-layouts: 38.6 us -> 26.1 us
    reshape x1 -> x0, local copies, waits for them, and re-layouts: 6.19 us -> none  [shards(): grad_cols = grad_cols.reshape(length, blk_devices, 1, piece_cols)]
    all_to_all x1 -> x0, local copies, waits for them, and re-layouts: 5.46 us -> none  [shards(): lax.all_to_all(grad_cols, 'seq', split_axis=0, concat_axis=2, tiled=True)]
  transfers between devices with their start and end apart: 5 -> 5, of which waited for: 4 -> 4; matrix products, arithmetic and copies ran while one was open for 15% -> 10% of each run, Pallas kernels for 0% -> 0%
where the time goes in v1:
time: 506 us; the launch traced here: 505 us
  blocking collectives  231 us (46%)
  waiting for transfers between devices  113 us (22%)
  matrix products  67.3 us (13%)
  local copies, waits for them, and re-layouts  45.6 us (9%)
  other arithmetic  30.1 us (6%)
  between operations  14 us (3%)
    all_to_all x2, blocking collectives, sum_at_owner(): lax.all_to_all(cut_along(shard, dim, length), axis, 0, 0, tiled=True)  106 us
    psum x1, blocking collectives, shards(): grad_gain = lax.psum(jnp.sum(grad_norm * scaled, axis=0), ('blk', 'seq'))  69.3 us
    all_gather x1, waiting for transfers between devices, shards(): grad_kv = lax.all_gather(grad_own, 'seq', axis=0, tiled=True)  51.5 us
    all_to_all x1, blocking collectives, shards(): lax.all_to_all(split_cols, 'seq', split_axis=2, concat_axis=0, tiled=True)  38.3 us
    all_gather x1, waiting for transfers between devices, shards(): kv_piece = lax.all_gather(kv_own, 'seq', axis=0, tiled=True)  30.3 us
    unnamed x29, local copies, waits for them, and re-layouts  26.1 us
    all_to_all x1, waiting for transfers between devices, test_columns(): jax.lax.all_to_all(d_next, concat_axis=0, split_axis=0, axis_name='seq')  22 us
    all_gather x1, blocking collectives, shards(): doc_piece = lax.all_gather(query_doc, 'seq', axis=0, tiled=True)  17 us
  transfers between devices with their start and end apart: 5, of which 4 were waited for; matrix products, arithmetic and copies ran while one was open for 10% of the time, Pallas kernels for 0%

profile of v1, /device:TPU:1, one launch (start us, length us, event | category | flops | bytes accessed | tf_op | source)
XLA Modules:
  0.0 505.3 jit_solution(345591463853602846)
XLA Ops:
  7.2 0.0 all-gather.5.cloned.1.call-start
  7.2 0.7 all-gather.5.cloned.1.call-update
  7.9 0.0 all-gather.7.cloned.1.call-start
  7.9 3.2 copy.51
  11.2 2.2 convert_element_type.135
  13.4 0.1 mul.121
  13.5 1.1 multiply_reduce_fusion
  14.6 2.9 multiply_convert_fusion
  17.5 0.2 copy.52
  17.7 38.3 %all_to_all.30 = bf16[128,16,8,64]{0,3,1,2:T(8,128)(2,1)} all-to-all(bf16[128,16,8,64]{0,3,1,2:T(8,128)(2,1)S(1)} %copy.52), channel_id=1, replica_groups=mesh['blk'=16,'seq'=8] {'seq'}, dimensions={2} | all-to-all | bytes 4194304 | tf_op jit(solution)/shard_map/all_to_all | solution.py:50
  56.0 8.3 %all-gather.5.cloned.1.call-done = bf16[1024,1024]{1,0:T(8,128)(2,1)} async-done(((bf16[64,1024]{1,0:T(8,128)(2,1)}), bf16[1024,1024]{1,0:T(8,128)(2,1)}) %all-gather.5.cloned.1.call-update) | async-done | bytes 2097168 | tf_op jit(solution)/shard_map/all_gather | solution.py:53
  64.3 4.6 fusion.25
  68.9 55.1 %all_to_all.31 = f32[8,128,1024]{2,1,0:T(8,128)} all-to-all(f32[8,128,1024]{2,1,0:T(8,128)S(1)} %fusion.25), channel_id=1, replica_groups=mesh['blk'=16,'seq'=8] {'seq'}, dimensions={0} | all-to-all | bytes 8388608 | tf_op jit(solution)/shard_map/all_to_all | solution.py:26
  124.0 3.4 reduce_sum.66
  127.5 0.0 all-gather.7.cloned.1.call-update
  127.5 0.0 all-gather.9.cloned.1.call-start
  127.6 1.2 copy.90
  128.8 2.3 copy.59
  131.0 17.0 %all-gather = s32[1,1024]{1,0:T(1,128)S(1)} all-gather(s32[1,128]{1,0:T(1,128)S(1)} %copy-done.6), channel_id=2, replica_groups=mesh['blk'=16,'seq'=8] {'seq'}, dimensions={1}, use_global_device_ids=true | all-gather | bytes 4608 | tf_op jit(solution)/shard_map/all_gather | solution.py:78
  148.1 0.2 fusion.32
  148.3 30.3 %all-gather.7.cloned.1.call-done = bf16[1024,1024]{1,0:T(8,128)(2,1)} async-done(((bf16[128,1024]{1,0:T(8,128)(2,1)}), bf16[1024,1024]{1,0:T(8,128)(2,1)}) %all-gather.7.cloned.1.call-update) | async-done | bytes 2097168 | tf_op jit(solution)/shard_map/all_gather | solution.py:77
  178.5 3.0 fusion.36
  181.5 1.5 copy.54
  183.0 9.1 %fusion.37 = (f32[4,8,128]{2,1,0:T(8,128)S(1)}, f32[4,8,128,1024]{2,3,1,0:T(8,128)}) fusion(bf16[1024,4,128,1]{0,2,3,1:T(8,128)(2,1)S(1)} %bitcast.121, bf16[128,4,8,128]{3,2,1,0:T(8,128)(2,1)} %bitcast.123, pred[128,1024]{0,1:T(8,128)(4,1)S(1)} %fusion.32), kind=kOutput, calls=%fused_computation.63 | convolution fusion | flops 1086320640 | bytes 19021824 | tf_op jit(solution)/shard_map/qgjd,kgd->gjqk/dot_general | solution.py:63
  192.1 2.3 copy.57
  194.4 8.7 %fusion.1 = f32[4,8,128]{2,1,0:T(8,128)S(1)} fusion(f32[4,8,128,1024]{2,3,1,0:T(8,128)} %get-tuple-element.33, f32[4,8,128]{2,1,0:T(8,128)S(1)} %broadcast_maximum_fusion, pred[128,1024]{0,1:T(8,128)(4,1)S(1)} %fusion.32), kind=kLoop, calls=%fused_computation.5 | loop fusion | flops 12578816 | bytes 16941056 | tf_op jit(solution)/shard_map/reduce_sum | solution.py:86
  203.1 9.9 %fusion.24 = (bf16[128,4,8,128]{0,3,2,1:T(8,128)(2,1)}, f32[4,8,128,128]{2,3,1,0:T(8,128)S(1)}) fusion(f32[128,4,8]{0,2,1:T(8,128)S(1)} %bitcast.146, bf16[1024,4,128,1]{0,2,3,1:T(8,128)(2,1)S(1)} %bitcast.144, f32[4,8,128,1024]{2,3,1,0:T(8,128)} %get-tuple-element.33, f32[4,8,128]{2,1,0:T(8,128)S(1)} %broadcast_maximum_fusion, ...), kind=kOutput, calls=%fused_computation.34 | convolution fusion | flops 1087373312 | bytes 21135360 | tf_op jit(solution)/shard_map/gjqk,kgd->gjqd/dot_general | solution.py:85
  212.9 0.5 multiply_reduce_fusion.1
  213.4 9.5 %fusion.27 = f32[1024,4,128]{2,0,1:T(8,128)} fusion(bf16[4,8,128,128]{2,3,1,0:T(8,128)(2,1)S(1)} %bitcast.130, f32[4,8,128,1024]{2,3,1,0:T(8,128)} %get-tuple-element.33, f32[4,8,128]{2,1,0:T(8,128)S(1)} %log_add_fusion, pred[128,1024]{0,1:T(8,128)(4,1)S(1)} %fusion.32), kind=kOutput, calls=%fused_computation.41 | convolution fusion | flops 1086324736 | bytes 20070400 | tf_op jit(solution)/shard_map/gjqk,gjqd->kgd/dot_general | solution.py:104
  222.9 10.3 %fusion = bf16[4,8,128,1024]{2,3,1,0:T(8,128)(2,1)} fusion(f32[4,8,128,1024]{2,3,1,0:T(8,128)} %get-tuple-element.33, bf16[1024,4,128,1]{0,2,3,1:T(8,128)(2,1)S(1)} %bitcast.145, bf16[4,8,128,128]{2,3,1,0:T(8,128)(2,1)S(1)} %bitcast.131, f32[4,8,128]{2,1,0:T(8,128)S(1)} %multiply_reduce_fusion.1, f32[4,8,128]{2,1,0:T(8,128)S(1)} %log_add_fusion, ...), kind=kOutput, calls=%fused_computation.1 | convolution fusion | flops 1094713344 | bytes 27426816 | tf_op jit(solution)/shard_map/gjqd,kgd->gjqk/dot_general | solution.py:101
  233.3 2.9 copy.66
  236.2 3.5 copy.92
  239.7 7.1 %fusion.23 = f32[1024,4,128]{2,0,1:T(8,128)} fusion(bf16[4,8,128,1024]{2,3,1,0:T(8,128)(2,1)} %fusion, bf16[128,4,8,128]{3,2,1,0:T(8,128)(2,1)S(1)} %bitcast.124), kind=kOutput, calls=%fused_computation.32 | convolution fusion | flops 1074266112 | bytes 11534336 | tf_op jit(solution)/shard_map/gjqk,qgjd->kgd/dot_general | solution.py:106
  246.8 2.9 copy.64
  249.6 2.2 copy.91
  251.9 0.3 pad_maximum_fusion
  252.1 0.8 copy.67
  253.0 50.9 %all_to_all.32 = f32[8,128,1024]{1,2,0:T(8,128)} all-to-all(f32[8,128,1024]{1,2,0:T(8,128)S(1)} %copy.67), channel_id=1, replica_groups=mesh['blk'=16,'seq'=8] {'seq'}, dimensions={0} | all-to-all | bytes 8388608 | tf_op jit(solution)/shard_map/all_to_all | solution.py:26
  303.9 3.2 reduce_sum.69
  307.1 0.0 all-gather.9.cloned.1.call-update
  307.1 0.3 reduce-scatter.2.cloned.1.call-start
  307.4 4.7 copy.70
  312.1 51.5 %all-gather.9.cloned.1.call-done = bf16[1024,1024]{0,1:T(8,128)(2,1)} async-done(((bf16[128,1024]{0,1:T(8,128)(2,1)}), bf16[1024,1024]{0,1:T(8,128)(2,1)}) %all-gather.9.cloned.1.call-update) | async-done | bytes 2097168 | tf_op jit(solution)/shard_map/all_gather | solution.py:119
  363.6 6.5 %fusion.20 = f32[1024,1024]{1,0:T(8,128)} fusion(bf16[1024,1024]{0,1:T(8,128)(2,1)} %all-gather.9.cloned.1.call-done, bf16[128,8,8,128]{3,2,1,0:T(8,128)(2,1)} %bitcast.133), kind=kOutput, calls=%fused_computation.28 | convolution fusion | flops 2147483648 | bytes 8388608 | tf_op jit(solution)/shard_map/dot_general | solution.py:123
  370.1 4.5 convolution_convert_fusion
  374.7 0.4 fusion.35
  375.1 0.7 constant_dynamic-update-slice_fusion.7
  375.8 0.7 constant_dynamic-update-slice_fusion.6
  376.5 0.7 constant_dynamic-update-slice_fusion.5
  377.2 0.7 constant_dynamic-update-slice_fusion.4
  378.0 0.7 constant_dynamic-update-slice_fusion.3
  378.7 0.7 constant_dynamic-update-slice_fusion.2
  379.4 0.7 constant_dynamic-update-slice_fusion.1
  380.1 0.7 constant_dynamic-update-slice_fusion
  380.8 4.3 all-to-all-start.3
  385.2 2.3 copy.71
  387.5 5.8 %multiply_convert_fusion.1 = bf16[4,128,8,128]{3,1,2,0:T(8,128)(2,1)} fusion(bf16[1024,4,128,1]{0,2,3,1:T(8,128)(2,1)S(1)} %bitcast.122, bf16[4,8,128,1024]{2,3,1,0:T(8,128)(2,1)} %fusion), kind=kOutput, calls=%fused_computation.37 | convolution fusion | flops 1074790400 | bytes 10485760 | tf_op jit(solution)/shard_map/gjqk,kgd->qgjd/dot_general | solution.py:110
  393.2 2.3 copy.72
  395.5 22.0 %all-to-all-done.3 = bf16[8,128,16,1,64]{1,4,2,3,0:T(8,128)(2,1)} async-done(((bf16[8,128,16,1,64]{1,4,2,3,0:T(8,128)(2,1)}), bf16[8,128,16,1,64]{1,4,2,3,0:T(8,128)(2,1)}, u32[]{:S(2)}, u32[]{:S(2)}) %all-to-all-start.3) | async-done | bytes 2097184 | tf_op jit(solution)/shard_map/all_to_all | solution.py:14
  417.5 4.3 fusion.17
  421.8 3.5 fusion.16
  425.3 4.1 copy.73
  429.4 0.1 reduce_sum.72
  429.4 69.3 %psum.7 = f32[8192]{0:T(1024)} all-reduce(f32[8192]{0:T(1024)S(1)} %reduce_sum.72), channel_id=1, replica_groups=mesh['blk'=16,'seq'=8] {'blk','seq'}, use_global_device_ids=true, to_apply=%region_9.10 | all-reduce | flops 8192 | bytes 65536 | tf_op jit(solution)/shard_map/psum | solution.py:134
  (21 shorter events, 0.1 us)
Async XLA Ops:
  7.2 57.1 %all-gather.5.cloned.1.call-start = ((), (), s32[]{:S(2)}) async-start(), calls=%async_computation.5 | async-start | bytes 2228224 | tf_op jit(solution)/shard_map/all_gather | solution.py:53
  7.9 170.6 %all-gather.7.cloned.1.call-start = ((), (), s32[]{:S(2)}) async-start(), calls=%async_computation.6 | async-start | bytes 2359296 | tf_op jit(solution)/shard_map/all_gather | solution.py:77
  11.2 2.3 copy-start.5
  124.0 3.5 copy-start.3
  127.5 236.1 %all-gather.9.cloned.1.call-start = ((), (), s32[]{:S(2)}) async-start(), calls=%async_computation.7 | async-start | bytes 2359296 | tf_op jit(solution)/shard_map/all_gather | solution.py:119
  127.6 3.5 copy-start.6
  194.4 8.7 %copy-start.4 = (bf16[1024,512]{0,1:T(8,128)(2,1)S(1)}, bf16[1024,512]{0,1:T(8,128)(2,1)}, u32[]{:S(2)}) copy-start(bf16[1024,512]{0,1:T(8,128)(2,1)} %copy.57) | copy-start | bytes 3145732
  203.1 9.9 %copy-start.2 = (bf16[1,128,4096]{1,2,0:T(8,128)(2,1)S(1)}, bf16[1,128,4096]{1,2,0:T(8,128)(2,1)}, u32[]{:S(2)}) copy-start(bf16[1,128,4096]{1,2,0:T(8,128)(2,1)} %copy.59) | copy-start | bytes 3145732
  236.2 3.5 copy-start
  249.6 2.2 copy-start.1
  307.1 191.6 %reduce-scatter.2.cloned.1.call-start = ((), (), s32[]{:S(2)}) async-start(), calls=%async_computation.8 | async-start | bytes 4456448 | tf_op jit(solution)/shard_map/reduce_scatter | solution.py:122
  380.8 36.7 %all-to-all-start.3 = ((bf16[8,128,16,1,64]{1,4,2,3,0:T(8,128)(2,1)}), bf16[8,128,16,1,64]{1,4,2,3,0:T(8,128)(2,1)}, u32[]{:S(2)}, u32[]{:S(2)}) async-start(bf16[8,128,16,1,64]{1,4,2,3,0:T(8,128)(2,1)} %constant_dynamic-update-slice_fusion), calls=%async_computation.3 | async-start | bytes 4194304 | tf_op jit(solution)/shard_map/all_to_all | solution.py:14
Sparse Core Ops, SparseCore 0:
  9.7 54.5 all-gather.4
  127.6 50.8 all-gather.6
  307.2 56.3 all-gather.8
  370.2 71.6 reduce-scatter.1
